TPU v7x, 256 devices: a whole 4x4x8 slice. The times are simulated.
256 devices in a mesh: row: 16 (over z, y_lo), col: 16 (over x, y_hi, core).
Axes of the slice: x: 4, y: 4 (y_hi: 2, y_lo: 2; y = y_hi * 2 + y_lo), z: 8, core: 2. Of those that a mesh axis runs over, the one named last changes fastest.
Arguments:
- matrix: float32 [12288, 12288], P('row', 'col'), may hold values from -30 to 30
- panels: float32 [2, 12288, 256], P(None, ('col', 'row')), may hold values from -0.0546875 to 0.0546875
- factors: float32 [2, 256, 256], replicated, may hold values from -1 to 2, as said below
Outputs:
- reduced: float32 [12288, 12288], P('row', 'col')
Inputs may be any that keep to these rules, and one draw needn't show every extreme that they name: Each factors[s] is upper triangular with diagonal entries between 1 and 2.
All inputs are finite; a program needn't handle non-finite values.
Results may differ from a plain program's by a relative error of at most 0.0003.
Values sent between devices are 32-bit elements; how exact they have to be, the bound alone decides.
A program may use at most 64 MiB of HBM per device.

v0:
```python
import jax
import jax.numpy as jnp
from jax import lax
from jax.sharding import PartitionSpec as P

highest = lax.Precision.HIGHEST


def laid_out(tiles, dim):
    dims = list(tiles.shape[1:])
    dims[dim] *= tiles.shape[0]
    return jnp.moveaxis(tiles, 0, dim).reshape(dims)


def from_everyone(value, axis):
    copies = jnp.broadcast_to(value, (lax.axis_size(axis), *value.shape))
    return lax.all_to_all(copies, axis, split_axis=0, concat_axis=0, tiled=True)


def gathered_copies(value, axis, dim):
    return laid_out(from_everyone(value, axis), dim)


def padded_to(lines, peers):
    spare = -len(lines) % peers
    return jnp.pad(lines, [(0, spare)] + [(0, 0)] * (lines.ndim - 1))


def broadcast_by_parts(value, axis, root):
    lines = jnp.where(lax.axis_index(axis) == root, value, jnp.zeros_like(value)).reshape(
        -1, *value.shape[1:][-1:]
    )
    padded = padded_to(lines, lax.axis_size(axis))
    own = lax.psum_scatter(padded, axis, scatter_dimension=0, tiled=True)
    return lax.all_gather(own, axis, axis=0, tiled=True)[: len(lines)].reshape(value.shape)


def cut_along(value, dim, peers):
    before, after = (value.shape[:dim], value.shape[dim + 1 :])
    return jnp.moveaxis(value.reshape(*before, peers, -1, *after), dim, 0)


def sent_and_summed(value, axis, dim):
    tiles = cut_along(value, dim, lax.axis_size(axis))
    arrived = lax.all_to_all(tiles, axis, split_axis=0, concat_axis=0, tiled=True)
    return arrived.sum(axis=0)


def nested_sum(value, axes):
    lines = value.reshape(-1, value.shape[-1])
    own = sent_and_summed(padded_to(lines, lax.axis_size(axes)), axes, 0)
    whole = gathered_copies(own, axes, 0)
    return whole[: len(lines)].reshape(value.shape)


def matmul(left, right):
    return jnp.dot(left, right, precision=highest, preferred_element_type=jnp.float32)


def transposed_product(left, right):
    return lax.dot_general(
        left, right, (((0,), (0,)), ((), ())), precision=highest, preferred_element_type=jnp.float32
    )


def outer_product(left, right):
    return lax.dot_general(
        left, right, (((1,), (1,)), ((), ())), precision=highest, preferred_element_type=jnp.float32
    )


def per_device(matrix, panels, factors):
    row_count = lax.axis_size("row")
    col_count = lax.axis_size("col")
    my_row = lax.axis_index("row")
    block_rows = matrix.shape[0]
    share = panels.shape[1]
    source = my_row * col_count // row_count
    offset = share * (my_row * col_count - source * row_count)
    gathered = gathered_copies(panels, "row", 1)
    relayed = broadcast_by_parts(gathered, "col", source)
    current = matrix
    for section in range(panels.shape[0]):
        factor = factors[section]
        panel_cols = gathered[section]
        panel_rows = relayed[section]
        sums_rows = nested_sum(matmul(current, panel_cols), "col")
        sums_cols = nested_sum(transposed_product(current, panel_rows), "row")
        image_rows = matmul(sums_rows, factor)
        image_cols = matmul(sums_cols, factor)
        inner = nested_sum(transposed_product(panel_rows, image_rows), "row")
        correction = transposed_product(factor, inner)
        update_rows = image_rows - 0.5 * matmul(panel_rows, correction)
        update_cols = image_cols - 0.5 * matmul(panel_cols, correction)
        current = (
            current
            - outer_product(panel_rows, update_cols)
            - outer_product(update_rows, panel_cols)
        )
    return current


def solution(mesh):
    return jax.shard_map(
        per_device,
        mesh=mesh,
        in_specs=(P("row", "col"), P(None, ("col", "row"), None), P()),
        out_specs=P("row", "col"),
        check_vma=False,
    )
```

profile of v0, /device:TPU:1, one launch (start us, length us, event | category | flops | bytes accessed | tf_op | source)
XLA Modules:
  0.0 425.3 jit_solution(6263676906609410572)
XLA Ops:
  8.7 10.1 %all-to-all-start = ((f32[16,2,48,256]{3,2,1,0:T(8,128)}), f32[16,2,48,256]{3,2,1,0:T(8,128)S(1)}, u32[]{:S(2)}, u32[]{:S(2)}) async-start(f32[16,2,48,256]{3,2,1,0:T(8,128)} %broadcast_in_dim.24), calls=%async_computation | async-start | bytes 3145728 | tf_op jit(solution)/shard_map/all_to_all | solution.py:17
  18.9 35.9 %all-to-all-done = f32[16,2,48,256]{3,2,1,0:T(8,128)S(1)} async-done(((f32[16,2,48,256]{3,2,1,0:T(8,128)}), f32[16,2,48,256]{3,2,1,0:T(8,128)S(1)}, u32[]{:S(2)}, u32[]{:S(2)}) %all-to-all-start) | async-done | bytes 1572896 | tf_op jit(solution)/shard_map/all_to_all | solution.py:17
  56.2 75.9 %reduce-scatter.2.cloned.1.call-done = f32[96,256]{1,0:T(8,128)} async-done(((f32[1536,256]{1,0:T(8,128)}), f32[96,256]{1,0:T(8,128)}) %reduce-scatter.2.cloned.1.call-update) | async-done | bytes 98320 | tf_op jit(solution)/shard_map/reduce_scatter | solution.py:34
  136.2 22.3 %all_to_all.65 = f32[16,48,256]{2,1,0:T(8,128)S(1)} all-to-all(f32[16,48,256]{2,1,0:T(8,128)S(1)} %fusion.38), channel_id=1, replica_groups=mesh['row'=16,'col'=16] {'col'}, dimensions={0} | all-to-all | bytes 1572864 | tf_op jit(solution)/shard_map/all_to_all | solution.py:45
  158.6 17.5 %all_to_all.66 = f32[16,48,256]{2,1,0:T(8,128)S(1)} all-to-all(f32[16,48,256]{2,1,0:T(8,128)S(1)} %broadcast_in_dim.27), channel_id=1, replica_groups=mesh['row'=16,'col'=16] {'col'}, dimensions={0} | all-to-all | bytes 1572864 | tf_op jit(solution)/shard_map/all_to_all | solution.py:17
  177.8 12.1 %all-gather.2.cloned.1.call-done = f32[1536,256]{1,0:T(8,128)} async-done(((f32[96,256]{1,0:T(8,128)}), f32[1536,256]{1,0:T(8,128)}) %all-gather.2.cloned.1.call-update) | async-done | bytes 1572880 | tf_op jit(solution)/shard_map/all_gather | solution.py:35
  193.5 6.9 %all-to-all-start.5 = ((f32[16,16,256]{2,1,0:T(8,128)}), f32[16,16,256]{2,1,0:T(8,128)S(1)}, u32[]{:S(2)}, u32[]{:S(2)}) async-start(f32[16,16,256]{2,1,0:T(8,128)} %bitcast.10), calls=%async_computation.6 | async-start | bytes 524288 | tf_op jit(solution)/shard_map/all_to_all | solution.py:45
  200.3 4.7 %convolution_bitcast_fusion = f32[768,256]{0,1:T(8,128)} fusion(f32[768,768]{1,0:T(8,128)} %param.3, f32[1536,256]{1,0:T(8,128)S(1)} %copy-done), kind=kOutput, calls=%fused_computation.3 | convolution fusion | flops 1811939328 | bytes 3932160 | tf_op jit(solution)/shard_map/dot_general | solution.py:61
  211.4 4.3 %all-to-all-start.1 = ((f32[16,48,256]{2,1,0:T(8,128)}), f32[16,48,256]{2,1,0:T(8,128)}, u32[]{:S(2)}, u32[]{:S(2)}) async-start(f32[16,48,256]{2,1,0:T(8,128)} %bitcast.86), calls=%async_computation.2 | async-start | bytes 1572864 | tf_op jit(solution)/shard_map/all_to_all | solution.py:45
  215.7 19.8 %all-to-all-done.1 = f32[16,48,256]{2,1,0:T(8,128)} async-done(((f32[16,48,256]{2,1,0:T(8,128)}), f32[16,48,256]{2,1,0:T(8,128)}, u32[]{:S(2)}, u32[]{:S(2)}) %all-to-all-start.1) | async-done | bytes 786464 | tf_op jit(solution)/shard_map/all_to_all | solution.py:45
  236.3 5.8 %all-to-all-start.6 = ((f32[16,16,256]{2,1,0:T(8,128)}), f32[16,16,256]{2,1,0:T(8,128)S(1)}, u32[]{:S(2)}, u32[]{:S(2)}) async-start(f32[16,16,256]{2,1,0:T(8,128)} %broadcast_in_dim.28), calls=%async_computation.7 | async-start | bytes 524288 | tf_op jit(solution)/shard_map/all_to_all | solution.py:17
  243.2 8.4 %all-to-all-done.6 = f32[16,16,256]{2,1,0:T(8,128)S(1)} async-done(((f32[16,16,256]{2,1,0:T(8,128)}), f32[16,16,256]{2,1,0:T(8,128)S(1)}, u32[]{:S(2)}, u32[]{:S(2)}) %all-to-all-start.6) | async-done | bytes 262176 | tf_op jit(solution)/shard_map/all_to_all | solution.py:17
  252.6 4.5 %all-to-all-start.2 = ((f32[16,48,256]{2,1,0:T(8,128)}), f32[16,48,256]{2,1,0:T(8,128)}, u32[]{:S(2)}, u32[]{:S(2)}) async-start(f32[16,48,256]{2,1,0:T(8,128)} %broadcast_in_dim.26), calls=%async_computation.3 | async-start | bytes 1572864 | tf_op jit(solution)/shard_map/all_to_all | solution.py:17
  261.6 14.8 %all-to-all-done.2 = f32[16,48,256]{2,1,0:T(8,128)} async-done(((f32[16,48,256]{2,1,0:T(8,128)}), f32[16,48,256]{2,1,0:T(8,128)}, u32[]{:S(2)}, u32[]{:S(2)}) %all-to-all-start.2) | async-done | bytes 786464 | tf_op jit(solution)/shard_map/all_to_all | solution.py:17
  285.9 24.4 %all_to_all.67 = f32[16,48,256]{2,1,0:T(8,128)} all-to-all(f32[16,48,256]{2,1,0:T(8,128)S(1)} %fusion.39), channel_id=1, replica_groups=mesh['row'=16,'col'=16] {'col'}, dimensions={0} | all-to-all | bytes 1572864 | tf_op jit(solution)/shard_map/all_to_all | solution.py:45
  311.6 17.5 %all_to_all.68 = f32[16,48,256]{2,1,0:T(8,128)S(1)} all-to-all(f32[16,48,256]{2,1,0:T(8,128)S(1)} %broadcast_in_dim.30), channel_id=1, replica_groups=mesh['row'=16,'col'=16] {'col'}, dimensions={0} | all-to-all | bytes 1572864 | tf_op jit(solution)/shard_map/all_to_all | solution.py:17
  335.6 5.9 %fusion.11 = f32[768,256]{1,0:T(8,128)} fusion(f32[768,768]{1,0:T(8,128)S(1)} %subtract_subtract_fusion.1, f32[1536,256]{1,0:T(8,128)} %all-gather.2.cloned.1.call-done), kind=kOutput, calls=%fused_computation.20 | convolution fusion | flops 1811939328 | bytes 3932160 | tf_op jit(solution)/shard_map/dot_general | solution.py:61
  341.4 5.4 %all-to-all-done.11 = f32[16,16,256]{2,1,0:T(8,128)S(1)} async-done(((f32[16,16,256]{2,1,0:T(8,128)}), f32[16,16,256]{2,1,0:T(8,128)S(1)}, u32[]{:S(2)}, u32[]{:S(2)}) %all-to-all-start.11) | async-done | bytes 262176 | tf_op jit(solution)/shard_map/all_to_all | solution.py:45
  346.9 4.3 %all-to-all-start.7 = ((f32[16,48,256]{2,1,0:T(8,128)}), f32[16,48,256]{2,1,0:T(8,128)}, u32[]{:S(2)}, u32[]{:S(2)}) async-start(f32[16,48,256]{2,1,0:T(8,128)} %bitcast.87), calls=%async_computation.8 | async-start | bytes 1572864 | tf_op jit(solution)/shard_map/all_to_all | solution.py:45
  351.2 19.2 %all-to-all-done.7 = f32[16,48,256]{2,1,0:T(8,128)} async-done(((f32[16,48,256]{2,1,0:T(8,128)}), f32[16,48,256]{2,1,0:T(8,128)}, u32[]{:S(2)}, u32[]{:S(2)}) %all-to-all-start.7) | async-done | bytes 786464 | tf_op jit(solution)/shard_map/all_to_all | solution.py:45
  371.1 6.2 %all-to-all-start.12 = ((f32[16,16,256]{2,1,0:T(8,128)}), f32[16,16,256]{2,1,0:T(8,128)S(1)}, u32[]{:S(2)}, u32[]{:S(2)}) async-start(f32[16,16,256]{2,1,0:T(8,128)} %broadcast_in_dim.31), calls=%async_computation.13 | async-start | bytes 524288 | tf_op jit(solution)/shard_map/all_to_all | solution.py:17
  378.5 8.4 %all-to-all-done.12 = f32[16,16,256]{2,1,0:T(8,128)S(1)} async-done(((f32[16,16,256]{2,1,0:T(8,128)}), f32[16,16,256]{2,1,0:T(8,128)S(1)}, u32[]{:S(2)}, u32[]{:S(2)}) %all-to-all-start.12) | async-done | bytes 262176 | tf_op jit(solution)/shard_map/all_to_all | solution.py:17
  387.9 4.5 %all-to-all-start.8 = ((f32[16,48,256]{2,1,0:T(8,128)}), f32[16,48,256]{2,1,0:T(8,128)}, u32[]{:S(2)}, u32[]{:S(2)}) async-start(f32[16,48,256]{2,1,0:T(8,128)} %broadcast_in_dim.29), calls=%async_computation.9 | async-start | bytes 1572864 | tf_op jit(solution)/shard_map/all_to_all | solution.py:17
  397.1 12.4 %all-to-all-done.8 = f32[16,48,256]{2,1,0:T(8,128)} async-done(((f32[16,48,256]{2,1,0:T(8,128)}), f32[16,48,256]{2,1,0:T(8,128)}, u32[]{:S(2)}, u32[]{:S(2)}) %all-to-all-start.8) | async-done | bytes 786464 | tf_op jit(solution)/shard_map/all_to_all | solution.py:17
  (69 shorter events, 60.5 us)
Async XLA Ops:
  8.7 46.1 %all-to-all-start = ((f32[16,2,48,256]{3,2,1,0:T(8,128)}), f32[16,2,48,256]{3,2,1,0:T(8,128)S(1)}, u32[]{:S(2)}, u32[]{:S(2)}) async-start(f32[16,2,48,256]{3,2,1,0:T(8,128)} %broadcast_in_dim.24), calls=%async_computation | async-start | bytes 3145728 | tf_op jit(solution)/shard_map/all_to_all | solution.py:17
  18.9 113.2 %reduce-scatter.2.cloned.1.call-start = ((), (), s32[]{:S(2)}) async-start(), calls=%async_computation.14 | async-start | bytes 1671168 | tf_op jit(solution)/shard_map/reduce_scatter | solution.py:34
  56.1 133.7 %all-gather.2.cloned.1.call-start = ((), (), s32[]{:S(2)}) async-start(), calls=%async_computation.15 | async-start | bytes 1671168 | tf_op jit(solution)/shard_map/all_gather | solution.py:35
  132.3 146.0 %copy-start.5 = (f32[1,16,48,256]{3,2,1,0:T(8,128)}, f32[1,16,48,256]{3,2,1,0:T(8,128)S(1)}, u32[]{:S(2)}) copy-start(f32[1,16,48,256]{3,2,1,0:T(8,128)S(1)} %get-tuple-element.6) | copy-start | bytes 2359300
  136.2 39.9 %copy-start.8 = (f32[2,256,256]{2,1,0:T(8,128)S(1)}, f32[2,256,256]{2,1,0:T(8,128)}, u32[]{:S(2)}) copy-start(f32[2,256,256]{2,1,0:T(8,128)} %param.5) | copy-start | bytes 1572868
  189.9 10.5 %copy-start = (f32[1536,256]{1,0:T(8,128)S(1)}, f32[1536,256]{1,0:T(8,128)}, u32[]{:S(2)}) copy-start(f32[1536,256]{1,0:T(8,128)} %all-gather.2.cloned.1.call-done) | copy-start | bytes 4718596
  193.5 18.0 %all-to-all-start.5 = ((f32[16,16,256]{2,1,0:T(8,128)}), f32[16,16,256]{2,1,0:T(8,128)S(1)}, u32[]{:S(2)}, u32[]{:S(2)}) async-start(f32[16,16,256]{2,1,0:T(8,128)} %bitcast.10), calls=%async_computation.6 | async-start | bytes 524288 | tf_op jit(solution)/shard_map/all_to_all | solution.py:45
  211.4 24.1 %all-to-all-start.1 = ((f32[16,48,256]{2,1,0:T(8,128)}), f32[16,48,256]{2,1,0:T(8,128)}, u32[]{:S(2)}, u32[]{:S(2)}) async-start(f32[16,48,256]{2,1,0:T(8,128)} %bitcast.86), calls=%async_computation.2 | async-start | bytes 1572864 | tf_op jit(solution)/shard_map/all_to_all | solution.py:45
  236.3 15.4 %all-to-all-start.6 = ((f32[16,16,256]{2,1,0:T(8,128)}), f32[16,16,256]{2,1,0:T(8,128)S(1)}, u32[]{:S(2)}, u32[]{:S(2)}) async-start(f32[16,16,256]{2,1,0:T(8,128)} %broadcast_in_dim.28), calls=%async_computation.7 | async-start | bytes 524288 | tf_op jit(solution)/shard_map/all_to_all | solution.py:17
  251.7 5.5 %copy-start.13 = (f32[16,16,256]{2,1,0:T(8,128)}, f32[16,16,256]{2,1,0:T(8,128)S(1)}, u32[]{:S(2)}) copy-start(f32[16,16,256]{2,1,0:T(8,128)S(1)} %all-to-all-done.6) | copy-start | bytes 786436
  252.6 23.8 %all-to-all-start.2 = ((f32[16,48,256]{2,1,0:T(8,128)}), f32[16,48,256]{2,1,0:T(8,128)}, u32[]{:S(2)}, u32[]{:S(2)}) async-start(f32[16,48,256]{2,1,0:T(8,128)} %broadcast_in_dim.26), calls=%async_computation.3 | async-start | bytes 1572864 | tf_op jit(solution)/shard_map/all_to_all | solution.py:17
  279.2 2.2 copy-start.4
  279.2 2.2 copy-start.6
  279.2 2.2 copy-start.11
  311.5 17.6 %copy-start.9 = (f32[2,256,256]{2,1,0:T(8,128)S(1)}, f32[2,256,256]{2,1,0:T(8,128)}, u32[]{:S(2)}) copy-start(f32[2,256,256]{2,1,0:T(8,128)} %param.5) | copy-start | bytes 1572868
  311.5 18.4 %copy-start.1 = (f32[1536,256]{1,0:T(8,128)S(1)}, f32[1536,256]{1,0:T(8,128)}, u32[]{:S(2)}) copy-start(f32[1536,256]{1,0:T(8,128)} %all-gather.2.cloned.1.call-done) | copy-start | bytes 4718596
  329.9 2.1 copy-start.7
  332.0 14.8 %all-to-all-start.11 = ((f32[16,16,256]{2,1,0:T(8,128)}), f32[16,16,256]{2,1,0:T(8,128)S(1)}, u32[]{:S(2)}, u32[]{:S(2)}) async-start(f32[16,16,256]{2,1,0:T(8,128)} %bitcast.20), calls=%async_computation.12 | async-start | bytes 524288 | tf_op jit(solution)/shard_map/all_to_all | solution.py:45
  346.9 23.5 %all-to-all-start.7 = ((f32[16,48,256]{2,1,0:T(8,128)}), f32[16,48,256]{2,1,0:T(8,128)}, u32[]{:S(2)}, u32[]{:S(2)}) async-start(f32[16,48,256]{2,1,0:T(8,128)} %bitcast.87), calls=%async_computation.8 | async-start | bytes 1572864 | tf_op jit(solution)/shard_map/all_to_all | solution.py:45
  371.1 15.8 %all-to-all-start.12 = ((f32[16,16,256]{2,1,0:T(8,128)}), f32[16,16,256]{2,1,0:T(8,128)S(1)}, u32[]{:S(2)}, u32[]{:S(2)}) async-start(f32[16,16,256]{2,1,0:T(8,128)} %broadcast_in_dim.31), calls=%async_computation.13 | async-start | bytes 524288 | tf_op jit(solution)/shard_map/all_to_all | solution.py:17
  386.9 5.5 %copy-start.12 = (f32[16,16,256]{2,1,0:T(8,128)}, f32[16,16,256]{2,1,0:T(8,128)S(1)}, u32[]{:S(2)}) copy-start(f32[16,16,256]{2,1,0:T(8,128)S(1)} %all-to-all-done.12) | copy-start | bytes 786436
  387.9 21.6 %all-to-all-start.8 = ((f32[16,48,256]{2,1,0:T(8,128)}), f32[16,48,256]{2,1,0:T(8,128)}, u32[]{:S(2)}, u32[]{:S(2)}) async-start(f32[16,48,256]{2,1,0:T(8,128)} %broadcast_in_dim.29), calls=%async_computation.9 | async-start | bytes 1572864 | tf_op jit(solution)/shard_map/all_to_all | solution.py:17
  409.5 2.9 copy-start.2
  412.4 2.2 copy-start.10
  (1 other events, 2.0 us)
Sparse Core Ops, SparseCore 0:
  56.3 75.7 reduce-scatter.1
  134.7 55.0 all-gather.1
where the time goes:
time: 433 us; the launch traced here: 425 us
  waiting for transfers between devices  216 us (50%)
  blocking collectives  81.7 us (19%)
  starting transfers between devices  50.2 us (12%)
  matrix products  48.2 us (11%)
  between operations  13.8 us (3%)
  local copies, waits for them, and re-layouts  10.1 us (2%)
  other arithmetic  4.93 us (1%)
    all_to_all x5, waiting for transfers between devices, from_everyone(): return lax.all_to_all(copies, axis, split_axis=0, concat_axis=0, tiled=True)  79.9 us
    reduce_scatter x1, waiting for transfers between devices, broadcast_by_parts(): own = lax.psum_scatter(padded, axis, scatter_dimension=0, tiled=True)  75.9 us
    all_to_all x4, waiting for transfers between devices, sent_and_summed(): lax.all_to_all(tiles, axis, split_axis=0, concat_axis=0, tiled=True)  48.5 us
    all_to_all x2, blocking collectives, sent_and_summed(): lax.all_to_all(tiles, axis, split_axis=0, concat_axis=0, tiled=True)  46.7 us
    all_to_all x2, blocking collectives, from_everyone(): return lax.all_to_all(copies, axis, split_axis=0, concat_axis=0, tiled=True)  35 us
    all_to_all x5, starting transfers between devices, from_everyone(): return lax.all_to_all(copies, axis, split_axis=0, concat_axis=0, tiled=True)  31.1 us
    dot_general x6, matrix products, transposed_product(): lax.dot_general(left, right, (((0,), (0,)), ((), ())), precision=highest,...  19.5 us
    all_to_all x4, starting transfers between devices, sent_and_summed(): lax.all_to_all(tiles, axis, split_axis=0, concat_axis=0, tiled=True)  19 us
  transfers between devices with their start and end apart: 11, of which 11 were waited for; matrix products, arithmetic and copies ran while one was open for 7% of the time, Pallas kernels for 0%

commit v1 on v0

v1 whole, which is shorter than its diff:
```python
import jax
import jax.numpy as jnp
from jax import lax
from jax.experimental import pallas as pl
from jax.experimental.pallas import tpu as pltpu
from jax.sharding import PartitionSpec as P

MESH = pl.DeviceIdType.MESH
HIGH = lax.Precision.HIGH
N = 16
SHARE = 48
B = 256
TILE = N * SHARE
HALF = TILE // 2
SEMS = 420


def nn(left, right):
    return jnp.dot(left, right, precision=HIGH, preferred_element_type=jnp.float32)


def tn(left, right):
    return lax.dot_general(
        left, right, (((0,), (0,)), ((), ())), precision=HIGH, preferred_element_type=jnp.float32
    )


def nt(left, right):
    return lax.dot_general(
        left, right, (((1,), (1,)), ((), ())), precision=HIGH, preferred_element_type=jnp.float32
    )


CHIPS = [(1, 0), (3, 0), (0, 1), (1, 1), (3, 1), (2, 0), (2, 1)]


def kernel(
    a_hbm, panels, f_ref, out_hbm,
    a, vc, vr, yc, yr, yp, d2d, rs, rx, gblk, gx, gall, gmat, mb, mx, mf, tc, sems,
):
    r = lax.axis_index("row")
    c = lax.axis_index("col")
    z, y = r // 2, r % 2
    x, yh, core = c // 4, (c // 2) % 2, c % 2
    chip = c // 2
    mate = (r, c + 1 - 2 * core)
    y_mate = (r + 1 - 2 * y, c)
    used = [0]

    def sem():
        used[0] += 1
        return sems.at[used[0] - 1]

    outgoing = []

    def send(src, dst, device):
        copy = pltpu.make_async_remote_copy(
            src_ref=src, dst_ref=dst, send_sem=sem(), recv_sem=sem(), device_id=device, device_id_type=MESH
        )
        copy.start()
        outgoing.append(copy)
        return copy

    def z_device(step):
        return (((z + step + 8) % 8) * 2 + y, c)

    def row_device(d):
        return ((r + d) % N, c)

    def chip_col(dx, dy):
        return ((x + dx) % 4) * 4 + ((yh + dy) % 2) * 2 + core

    def ring_start(buf):
        flight = {}
        for p in range(2):
            for way in (1, -1):
                flight[way, 1, 0, p] = send(buf.at[r, p], buf.at[r, p], z_device(way))
            flight[0, 0, 1, p] = send(buf.at[r, p], buf.at[r, p], y_mate)
        for p in range(2):
            flight[0, 0, 1, p].wait_recv()
            other = r + 1 - 2 * y
            for way in (1, -1):
                flight[way, 1, 1, p] = send(buf.at[other, p], buf.at[other, p], z_device(way))
        return flight

    def ring_step(buf, flight, k):
        for line in range(2):
            for p in range(2):
                for way in (1, -1):
                    if (way, k, line, p) not in flight:
                        continue
                    flight[way, k, line, p].wait_recv()
                    if k < 3 or (k == 3 and way == (1, -1)[line]):
                        block = ((z - way * k + 8) % 8) * 2 + (y if line == 0 else 1 - y)
                        flight[way, k + 1, line, p] = send(buf.at[block, p], buf.at[block, p], z_device(way))

    def col_start(buf):
        flight = {}
        for dx, dy in CHIPS:
            flight[dx, dy] = send(buf.at[c], buf.at[c], (r, chip_col(dx, dy)))
        flight["mate"] = [send(buf.at[c], buf.at[c], mate)]
        return flight

    def col_finish(buf, flight):
        for dx, dy in CHIPS:
            flight[dx, dy].wait_recv()
            block = chip_col(4 - dx, dy)
            flight["mate"].append(send(buf.at[block], buf.at[block], mate))
        for copy in flight["mate"]:
            copy.wait_recv()

    class Transpose:
        def __init__(self, src, dst):
            recv = sem()
            self.remote = pltpu.make_async_remote_copy(
                src_ref=src, dst_ref=dst, send_sem=sem(), recv_sem=recv, device_id=(c, r), device_id_type=MESH
            )
            self.local = pltpu.make_async_copy(src, dst, recv)

            @pl.when(r != c)
            def _():
                self.remote.start()

            @pl.when(r == c)
            def _():
                self.local.start()

        def wait(self):
            @pl.when(r != c)
            def _():
                self.remote.wait_recv()

            @pl.when(r == c)
            def _():
                self.local.wait()

        def drain(self):
            @pl.when(r != c)
            def _():
                self.remote.wait_send()

    own_panels = pltpu.make_async_copy(panels, vc.at[r], sem())
    own_panels.start()
    tile_in = pltpu.make_async_copy(a_hbm, a, sem())
    tile_in.start()

    barrier = pltpu.get_barrier_semaphore()
    for d in range(1, N):
        pl.semaphore_signal(barrier, inc=1, device_id=row_device(d), device_id_type=MESH)
        pl.semaphore_signal(barrier, inc=1, device_id=(r, (c + d) % N), device_id_type=MESH)

    @pl.when(r != c)
    def _():
        pl.semaphore_signal(barrier, inc=1, device_id=(c, r), device_id_type=MESH)
        pl.semaphore_wait(barrier, 2 * (N - 1) + 1)

    @pl.when(r == c)
    def _():
        pl.semaphore_wait(barrier, 2 * (N - 1))

    own_panels.wait()

    turned = Transpose(vc.at[r], vr.at[r])
    ring = ring_start(vc)
    ring_step(vc, ring, 1)
    turned.wait()
    rows_v = col_start(vr)
    for k in (2, 3, 4):
        ring_step(vc, ring, k)
    tile_in.wait()

    def panel(buf, p, first=0, count=N):
        return buf[first:first + count, p].reshape(count * SHARE, B)

    pair = []
    for h in range(2):
        for p in range(2):
            part = nn(a[h * HALF:(h + 1) * HALF, :], panel(vc, p)).reshape(4, 2, SHARE, B)
            yp[0, 4 * h:4 * h + 4, p] = part[:, 0]
            yp[1, 4 * h:4 * h + 4, p] = part[:, 1]
        pair.append(send(yp.at[1 - core, pl.ds(4 * h, 4)], d2d.at[pl.ds(4 * h, 4)], mate))

    left = vc[:, 0, :, pl.ds(pl.multiple_of((r % 2) * 128, 128), 128)].reshape(TILE, 128)
    right = vc[:, 1, :, pl.ds(pl.multiple_of(((r // 2) % 2) * 128, 128), 128)].reshape(TILE, 128)
    gblk[...] = tn(left, right).reshape(4, 32, 128)

    for h in range(2):
        pair[h].wait_recv()
        rs[4 * h:4 * h + 4] = yp[core, 4 * h:4 * h + 4] + d2d[4 * h:4 * h + 4]
    parts = []
    for i, (dx, dy) in enumerate(CHIPS):
        parts.append(send(rs.at[chip_col(dx, dy) // 2], rx.at[i], (r, chip_col(dx, dy))))
    g_parts = [send(gblk.at[r // 4], gx.at[d], (r, (c + d) % N)) for d in range(1, N)]
    col_finish(vr, rows_v)
    for copy in g_parts:
        copy.wait_recv()
    total = gblk[r // 4]
    for d in range(1, N):
        total += gx[d]
    gall[r] = total
    g_all = [send(gall.at[r], gall.at[r], row_device(d)) for d in range(1, N)]
    for copy in g_all:
        copy.wait_recv()
    for i in range(N):
        bi, bj, s = i % 2, (i // 2) % 2, i // 4
        gmat[128 * bi + 32 * s:128 * bi + 32 * s + 32, 128 * bj:128 * bj + 128] = gall[i]

    f1, f2 = f_ref[0], f_ref[1]
    gf2 = nn(gmat[...], f2)
    for copy in parts:
        copy.wait_recv()
    y1 = rs[chip, 0]
    y2 = rs[chip, 1]
    for i in range(len(CHIPS)):
        y1 += rx[i, 0]
        y2 += rx[i, 1]
    first = nn(y1, f1)
    yr[c, 0] = first
    yr[c, 1] = nn(y2, f2) - nn(first, gf2)

    turned_y = Transpose(yr.at[c], yc.at[c])
    rows_y = col_start(yr)
    turned_y.wait()
    ring = ring_start(yc)
    col_finish(yr, rows_y)

    left = vr[:, (chip // 2 + 2) // 3, :, pl.ds(pl.multiple_of(core * 128, 128), 128)].reshape(TILE, 128)
    right = yr[:, chip // 4, :, pl.ds(pl.multiple_of((chip % 2) * 128, 128), 128)].reshape(TILE, 128)
    mb[...] = tn(left, right).reshape(N, 8, 128)
    m_parts = [send(mb.at[(r + d) % N], mx.at[d], row_device(d)) for d in range(1, N)]
    ring_step(yc, ring, 1)
    for copy in m_parts:
        copy.wait_recv()
    total = mb[r]
    for d in range(1, N):
        total += mx[d]
    mf[c, r] = total
    m_all = [send(mf.at[c, r], mf.at[c, r], row_device(d)) for d in range(1, N)]
    ring_step(yc, ring, 2)
    for copy in m_all:
        copy.wait_recv()
    rows_m = col_start(mf)
    ring_step(yc, ring, 3)
    for h in range(2):
        rows = slice(h * HALF, (h + 1) * HALF)
        a[rows, :] -= nt(panel(yr, 0, 8 * h, 8), panel(vc, 0)) + nt(panel(yr, 1, 8 * h, 8), panel(vc, 1))
    ring_step(yc, ring, 4)
    col_finish(mf, rows_m)

    def block(i):
        def part(q, k):
            return mf[2 * q + k].reshape(128, 128)

        return jnp.concatenate(
            [jnp.concatenate([part(2 * i, k), part(2 * i + 1, k)], axis=1) for k in range(2)], axis=0
        )

    g = gmat[...]
    k1 = tn(f1, block(0))
    h_mat = block(1).T - 0.5 * tn(k1, g)
    l_mat = nn(h_mat - 0.5 * nn(k1, g), f2)
    k2 = tn(f2, block(2) - tn(g, l_mat))
    r11 = -0.5 * (k1 + k1.T)
    r22 = -0.5 * (k2 + k2.T)
    v1, v2 = panel(vc, 0), panel(vc, 1)
    tc[0] = panel(yc, 0) + nn(v1, r11) - nt(v2, l_mat)
    tc[1] = panel(yc, 1) - nn(v1, l_mat) + nn(v2, r22)
    out_copies = []
    for h in range(2):
        rows = slice(h * HALF, (h + 1) * HALF)
        a[rows, :] -= nt(panel(vr, 0, 8 * h, 8), tc[0]) + nt(panel(vr, 1, 8 * h, 8), tc[1])
        copy = pltpu.make_async_copy(a.at[pl.ds(h * HALF, HALF)], out_hbm.at[pl.ds(h * HALF, HALF)], sem())
        copy.start()
        out_copies.append(copy)
    for copy in outgoing:
        copy.wait_send()
    turned.drain()
    turned_y.drain()
    for copy in out_copies:
        copy.wait()
    assert used[0] <= SEMS


def per_device(matrix, panels, factors):
    f32 = jnp.float32
    blocks = pltpu.VMEM((N, 2, SHARE, B), f32)
    return pl.pallas_call(
        kernel,
        out_shape=jax.ShapeDtypeStruct((TILE, TILE), f32),
        in_specs=[
            pl.BlockSpec(memory_space=pl.ANY),
            pl.BlockSpec(memory_space=pl.ANY),
            pl.BlockSpec(memory_space=pltpu.VMEM),
        ],
        out_specs=pl.BlockSpec(memory_space=pl.ANY),
        scratch_shapes=[
            pltpu.VMEM((TILE, TILE), f32),
            blocks,
            blocks,
            blocks,
            blocks,
            pltpu.VMEM((2, 8, 2, SHARE, B), f32),
            pltpu.VMEM((8, 2, SHARE, B), f32),
            pltpu.VMEM((8, 2, SHARE, B), f32),
            pltpu.VMEM((7, 2, SHARE, B), f32),
            pltpu.VMEM((4, 32, 128), f32),
            pltpu.VMEM((N, 32, 128), f32),
            pltpu.VMEM((N, 32, 128), f32),
            pltpu.VMEM((B, B), f32),
            pltpu.VMEM((N, 8, 128), f32),
            pltpu.VMEM((N, 8, 128), f32),
            pltpu.VMEM((N, N, 8, 128), f32),
            pltpu.VMEM((2, TILE, B), f32),
            pltpu.SemaphoreType.DMA((SEMS,)),
        ],
        compiler_params=pltpu.CompilerParams(
            collective_id=0, has_side_effects=True, vmem_limit_bytes=60 * 1024 * 1024
        ),
    )(matrix, panels, factors)


def solution(mesh):
    return jax.shard_map(
        per_device,
        mesh=mesh,
        in_specs=(P("row", "col"), P(None, ("col", "row"), None), P()),
        out_specs=P("row", "col"),
        check_vma=False,
    )
```

time: 433 us -> 122 us (0.28); the launches traced: 425 us -> 121 us
  waiting for transfers between devices: 216 us -> 0 us
  Pallas kernels: 0 us -> 118 us
  blocking collectives: 81.7 us -> 0 us
  starting transfers between devices: 50.2 us -> 0 us
  matrix products: 48.2 us -> 0 us
  between operations: 13.8 us -> 0.01 us
  local copies, waits for them, and re-layouts: 10.1 us -> 3.22 us
  other arithmetic: 4.93 us -> 0 us
    all_to_all x9 -> x0, waiting for transfers between devices: 128 us -> none  [the longest x5 79.9 us: from_everyone(): return lax.all_to_all(copies, axis, split_axis=0, concat_axis=0, tiled=True)]
    pallas_call x0 -> x1, Pallas kernels: none -> 118 us  [per_device(): pl.pallas_call(kernel, out_shape=jax.ShapeDtypeStruct((TILE, TILE), f32),...]
    all_to_all x4 -> x0, blocking collectives: 81.7 us -> none  [the longest x2 46.7 us: sent_and_summed(): lax.all_to_all(tiles, axis, split_axis=0, concat_axis=0, tiled=True)]
    reduce_scatter x1 -> x0, waiting for transfers between devices: 75.9 us -> none  [broadcast_by_parts(): own = lax.psum_scatter(padded, axis, scatter_dimension=0, tiled=True)]
    all_to_all x9 -> x0, starting transfers between devices: 50.1 us -> none  [the longest x5 31.1 us: from_everyone(): return lax.all_to_all(copies, axis, split_axis=0, concat_axis=0, tiled=True)]
    dot_general x20 -> x0, matrix products: 48.2 us -> none  [the longest x6 19.5 us: transposed_product(): lax.dot_general(left, right, (((0,), (0,)), ((), ())), precision=highest,...]
    all_gather x1 -> x0, waiting for transfers between devices: 12.1 us -> none  [broadcast_by_parts(): lax.all_gather(own, axis, axis=0, tiled=True)[:len(lines)]]
    broadcast_in_dim x7 -> x0, local copies, waits for them, and re-layouts: 5.73 us -> none  [from_everyone(): copies = jnp.broadcast_to(value, (lax.axis_size(axis), *value.shape))]
  transfers between devices with their start and end apart: 11 -> 0, of which waited for: 11 -> 0; matrix products, arithmetic and copies ran while one was open for 7% -> 0% of each run, Pallas kernels for 0% -> 0%
where the time goes in v1:
time: 122 us; the launch traced here: 121 us
  Pallas kernels  118 us (97%)
  local copies, waits for them, and re-layouts  3.22 us (3%)
    pallas_call x1, Pallas kernels, per_device(): pl.pallas_call(kernel, out_shape=jax.ShapeDtypeStruct((TILE, TILE), f32),...  118 us
    unnamed x1, local copies, waits for them, and re-layouts  3.22 us

profile of v1, /device:TPU:1, one launch (start us, length us, event | category | flops | bytes accessed | tf_op | source)
XLA Modules:
  0.0 121.4 jit_solution(7635028059703181025)
XLA Ops:
  0.0 118.2 %shard_map.37 = f32[768,768]{1,0:T(8,128)} custom-call(f32[768,768]{1,0:T(8,128)} %a_hbm.1, f32[2,48,256]{2,1,0:T(8,128)} %panels.1, f32[2,256,256]{2,1,0:T(8,128)} %f_ref.1), custom_call_target="tpu_custom_call" | custom-call | tf_op jit(solution)/shard_map/pallas_call | solution.py:287
  118.2 3.2 %copy.5 = f32[768,768]{1,0:T(8,128)} copy(f32[768,768]{1,0:T(8,128)} %shard_map.37) | data formatting | bytes 4718592

commit v2 on v1

v2 whole, which is shorter than its diff:
```python
import jax
import jax.numpy as jnp
from jax import lax
from jax.experimental import pallas as pl
from jax.experimental.pallas import tpu as pltpu
from jax.sharding import PartitionSpec as P

MESH = pl.DeviceIdType.MESH
HIGH = lax.Precision.HIGH
N = 16
SHARE = 48
B = 256
TILE = N * SHARE
HALF = TILE // 2
SEMS = 540


def nn(left, right):
    return jnp.dot(left, right, precision=HIGH, preferred_element_type=jnp.float32)


def tn(left, right):
    return lax.dot_general(
        left, right, (((0,), (0,)), ((), ())), precision=HIGH, preferred_element_type=jnp.float32
    )


def nt(left, right):
    return lax.dot_general(
        left, right, (((1,), (1,)), ((), ())), precision=HIGH, preferred_element_type=jnp.float32
    )


NEAR = (1, 2)
CHIPS = [(1, 0), (3, 0), (0, 1), (1, 1), (3, 1), (2, 0), (2, 1)]


def kernel(
    a_hbm, panels, f_hbm, out,
    a, vc, vr, yc, yr, yp, d2d, rs, rx, gblk, gx, gall, gmat, ym, yx, mb, mx, mf, tc, f_ref, sems,
):
    r = lax.axis_index("row")
    c = lax.axis_index("col")
    z, y = r // 2, r % 2
    x, yh, core = c // 4, (c // 2) % 2, c % 2
    chip = c // 2
    mate = (r, c + 1 - 2 * core)
    y_mate = (r + 1 - 2 * y, c)
    used = [0]

    def sem():
        used[0] += 1
        return sems.at[used[0] - 1]

    outgoing = []

    def send(src, dst, device):
        copy = pltpu.make_async_remote_copy(
            src_ref=src, dst_ref=dst, send_sem=sem(), recv_sem=sem(), device_id=device, device_id_type=MESH
        )
        copy.start()
        outgoing.append(copy)
        return copy

    def z_device(step):
        return (((z + step + 8) % 8) * 2 + y, c)

    def row_device(d):
        return ((r + d) % N, c)

    def chip_at(dx, dy):
        return ((x + dx) % 4) * 2 + (yh + dy) % 2

    def block_at(way, k, line):
        return ((z - way * k + 8) % 8) * 2 + (y if line == 0 else 1 - y)

    def ring_start(buf, flight, p):
        for way in (1, -1):
            flight[way, 1, 0, p] = send(buf.at[r, p], buf.at[r, p], z_device(way))
        flight[0, p] = send(buf.at[r, p], buf.at[r, p], y_mate)

    def ring_mates(buf, flight, seen):
        other = r + 1 - 2 * y
        for p in range(2):
            flight[0, p].wait_recv()
            for way in (1, -1):
                flight[way, 1, 1, p] = send(buf.at[other, p], buf.at[other, p], z_device(way))
            seen(other, p)

    def ring_step(buf, flight, k, seen):
        for line in range(2):
            for p in range(2):
                for way in (1, -1):
                    if (way, k, line, p) not in flight:
                        continue
                    flight[way, k, line, p].wait_recv()
                    at = block_at(way, k, line)
                    if line:
                        on = k < NEAR[p]
                    else:
                        on = k < 3 or (k == 3 and way == (1, -1)[p])
                    if on:
                        flight[way, k + 1, line, p] = send(buf.at[at, p], buf.at[at, p], z_device(way))
                    if line == 0 and k > NEAR[p]:
                        flight["y", way, k, p] = send(buf.at[at, p], buf.at[at, p], y_mate)
                    seen(at, p)

    def ring_finish(flight, seen):
        for key in flight:
            if key[0] == "y":
                flight[key].wait_recv()
                seen(block_at(key[1], key[2], 1), key[3])

    def unseen(at, p):
        pass

    def col_start(buf, part=None):
        def at(chip_index):
            return buf.at[chip_index, core] if part is None else buf.at[chip_index, core, part]

        flight = [send(at(chip), at(chip), (r, chip_at(dx, dy) * 2 + core)) for dx, dy in CHIPS]
        return at, flight, [send(at(chip), at(chip), mate)]

    def col_forward(state):
        at, flight, mates = state
        for (dx, dy), copy in zip(CHIPS, flight):
            copy.wait_recv()
            source = chip_at(4 - dx, dy)
            mates.append(send(at(source), at(source), mate))

    def col_finish(state):
        for copy in state[2]:
            copy.wait_recv()

    class Transpose:
        def __init__(self, src, dst):
            recv = sem()
            self.remote = pltpu.make_async_remote_copy(
                src_ref=src, dst_ref=dst, send_sem=sem(), recv_sem=recv, device_id=(c, r), device_id_type=MESH
            )
            self.local = pltpu.make_async_copy(src, dst, recv)

            @pl.when(r != c)
            def _():
                self.remote.start()

            @pl.when(r == c)
            def _():
                self.local.start()

        def wait(self):
            @pl.when(r != c)
            def _():
                self.remote.wait_recv()

            @pl.when(r == c)
            def _():
                self.local.wait()

        def drain(self):
            @pl.when(r != c)
            def _():
                self.remote.wait_send()

    def finish():
        for copy in outgoing:
            copy.wait_send()
        for item in turned:
            item.drain()

        @pl.when(r == c)
        def _():
            for copy in handed:
                copy.wait_send()

    own_panels = pltpu.make_async_copy(panels, vc.at[r], sem())
    own_panels.start()
    factors_in = pltpu.make_async_copy(f_hbm, f_ref, sem())
    factors_in.start()
    tile_in = pltpu.make_async_copy(a_hbm, a, sem())
    tile_in.start()

    barrier = pltpu.get_barrier_semaphore()
    for device in [z_device(1), z_device(-1), y_mate] + [(r, (c + d) % N) for d in range(1, N)]:
        pl.semaphore_signal(barrier, inc=1, device_id=device, device_id_type=MESH)
    pl.semaphore_wait(barrier, 3 + N - 1)

    own_panels.wait()

    turned = []
    handed = []
    hand_recv = [sem(), sem()]
    own_rows = [pltpu.make_async_copy(vc.at[r, p], vr.at[chip, core, p], hand_recv[p]) for p in range(2)]

    @pl.when(r == c)
    def _():
        for copy in own_rows:
            copy.start()

    def hand(at, p):
        copy = pltpu.make_async_remote_copy(
            src_ref=vc.at[at, p], dst_ref=vr.at[at // 2, at % 2, p], send_sem=sem(), recv_sem=hand_recv[p],
            device_id=(r, at), device_id_type=MESH,
        )
        handed.append(copy)

        @pl.when(r == c)
        def _():
            copy.start()

    ring = {}
    for p in range(2):
        ring_start(vc, ring, p)
    ring_mates(vc, ring, hand)
    for k in (1, 2, 3, 4):
        ring_step(vc, ring, k, hand)
    ring_finish(ring, hand)
    tile_in.wait()
    factors_in.wait()

    def panel(p):
        return vc[:, p].reshape(TILE, B)

    def row_panel(buf, p, h):
        return buf[4 * h:4 * h + 4, :, p].reshape(HALF, B)

    left = vc[:, 0, :, pl.ds(pl.multiple_of((r % 2) * 128, 128), 128)].reshape(TILE, 128)
    right = vc[:, 1, :, pl.ds(pl.multiple_of(((r // 2) % 2) * 128, 128), 128)].reshape(TILE, 128)
    gblk[...] = tn(left, right).reshape(4, 32, 128)
    g_parts = [send(gblk.at[r // 4], gx.at[d], (r, (c + d) % N)) for d in range(1, N)]

    pair = []
    for p in range(2):
        for h in range(2):
            part = nn(a[h * HALF:(h + 1) * HALF, :], panel(p)).reshape(4, 2, SHARE, B)
            yp[p, 0, 4 * h:4 * h + 4] = part[:, 0]
            yp[p, 1, 4 * h:4 * h + 4] = part[:, 1]
        pair.append(send(yp.at[p, 1 - core], d2d.at[p], mate))
    parts = []
    for p in range(2):
        pair[p].wait_recv()
        rs[p] = yp[p, core] + d2d[p]
        for i, (dx, dy) in enumerate(CHIPS):
            parts.append(send(rs.at[p, chip_at(dx, dy)], rx.at[p, i], (r, chip_at(dx, dy) * 2 + core)))
    for copy in g_parts:
        copy.wait_recv()
    total = gblk[r // 4]
    for d in range(1, N):
        total += gx[d]
    gall[r] = total
    g_all = [send(gall.at[r], gall.at[r], row_device(d)) for d in range(1, N)]
    for copy in own_rows:
        copy.wait()
    rows_v = col_start(vr)
    for copy in g_all:
        copy.wait_recv()
    for i in range(N):
        bi, bj, s = i % 2, (i // 2) % 2, i // 4
        gmat[128 * bi + 32 * s:128 * bi + 32 * s + 32, 128 * bj:128 * bj + 128] = gall[i]
    f1, f2 = f_ref[0], f_ref[1]
    gf2 = nn(gmat[...], f2)

    def summed(p):
        for copy in parts[p * len(CHIPS):(p + 1) * len(CHIPS)]:
            copy.wait_recv()
        total = rs[p, chip]
        for i in range(len(CHIPS)):
            total += rx[p, i]
        return total

    first = nn(summed(0), f1)
    yr[chip, core, 0] = first
    turned_y = [Transpose(yr.at[chip, core, 0], yc.at[c, 0])]
    second = nn(summed(1), f2) - nn(first, gf2)
    yr[chip, core, 1] = second
    turned_y.append(Transpose(yr.at[chip, core, 1], yc.at[c, 1]))
    turned += turned_y
    for w, value in enumerate((first, second)):
        for half in range(2):
            ym[2 * w + half] = value[:, 128 * half:128 * half + 128]

    slices = []
    for dx, dy in CHIPS:
        other = chip_at(dx, dy)
        slices.append(send(ym.at[(other // 4) * 2 + other % 2], yx.at[chip], (r, other * 2 + core)))
    yx[chip] = ym[(chip // 4) * 2 + chip % 2]
    for copy in slices:
        copy.wait_recv()
    col_forward(rows_v)
    left = vr[:, core, (chip // 2 + 2) // 3].reshape(HALF, B)
    mb[...] = tn(left, yx[...].reshape(HALF, 128)).reshape(2, N, 8, 128)
    m_parts = []
    for d in range(N):
        for k in range(2):
            if d or k:
                row, other = (r + d) % N, (core + k) % 2
                m_parts.append(send(mb.at[other, row], mx.at[core, r], (row, chip * 2 + other)))
    mx[core, r] = mb[core, r]
    ring = {}
    for p in range(2):
        turned_y[p].wait()
        ring_start(yc, ring, p)
    rows_y = [col_start(yr, p) for p in range(2)]
    for copy in m_parts:
        copy.wait_recv()
    mf[chip, core, r] = mx[...].reshape(2 * N, 8, 128).sum(axis=0)
    m_all = [send(mf.at[chip, core, r], mf.at[chip, core, r], row_device(d)) for d in range(1, N)]
    ring_mates(yc, ring, unseen)
    ring_step(yc, ring, 1, unseen)
    for copy in m_all:
        copy.wait_recv()
    rows_m = col_start(mf)
    ring_step(yc, ring, 2, unseen)
    for state in rows_y:
        col_forward(state)
    ring_step(yc, ring, 3, unseen)
    col_forward(rows_m)
    ring_step(yc, ring, 4, unseen)
    for state in [rows_v] + rows_y:
        col_finish(state)
    for h in range(2):
        rows = slice(h * HALF, (h + 1) * HALF)
        a[rows, :] -= nt(row_panel(yr, 0, h), panel(0)) + nt(row_panel(yr, 1, h), panel(1))
    col_finish(rows_m)

    def block(i):
        return jnp.concatenate([mf[2 * i].reshape(B, 128), mf[2 * i + 1].reshape(B, 128)], axis=1)

    g = gmat[...]
    k1 = tn(f1, block(0))
    h_mat = block(1).T - 0.5 * tn(k1, g)
    l_mat = nn(h_mat - 0.5 * nn(k1, g), f2)
    k2 = tn(f2, block(2) - tn(g, l_mat))
    r11 = -0.5 * (k1 + k1.T)
    r22 = -0.5 * (k2 + k2.T)
    v1, v2 = panel(0), panel(1)
    tc[0] = nn(v1, r11) - nt(v2, l_mat)
    tc[1] = nn(v2, r22) - nn(v1, l_mat)
    ring_finish(ring, unseen)
    for p in range(2):
        tc[p] += yc[:, p].reshape(TILE, B)
    for h in range(2):
        rows = slice(h * HALF, (h + 1) * HALF)
        out[rows, :] = a[rows, :] - (nt(row_panel(vr, 0, h), tc[0]) + nt(row_panel(vr, 1, h), tc[1]))
    finish()
    assert used[0] <= SEMS


def per_device(matrix, panels, factors):
    f32 = jnp.float32
    blocks = pltpu.VMEM((N, 2, SHARE, B), f32)
    row_blocks = pltpu.VMEM((8, 2, 2, SHARE, B), f32)
    return pl.pallas_call(
        kernel,
        out_shape=jax.ShapeDtypeStruct((TILE, TILE), f32),
        in_specs=[
            pl.BlockSpec(memory_space=pltpu.HBM),
            pl.BlockSpec(memory_space=pltpu.HBM),
            pl.BlockSpec(memory_space=pltpu.HBM),
        ],
        out_specs=pl.BlockSpec(memory_space=pltpu.VMEM),
        scratch_shapes=[
            pltpu.VMEM((TILE, TILE), f32),
            blocks,
            row_blocks,
            blocks,
            row_blocks,
            pltpu.VMEM((2, 2, 8, SHARE, B), f32),
            pltpu.VMEM((2, 8, SHARE, B), f32),
            pltpu.VMEM((2, 8, SHARE, B), f32),
            pltpu.VMEM((2, 7, SHARE, B), f32),
            pltpu.VMEM((4, 32, 128), f32),
            pltpu.VMEM((N, 32, 128), f32),
            pltpu.VMEM((N, 32, 128), f32),
            pltpu.VMEM((B, B), f32),
            pltpu.VMEM((4, SHARE, 128), f32),
            pltpu.VMEM((8, SHARE, 128), f32),
            pltpu.VMEM((2, N, 8, 128), f32),
            pltpu.VMEM((2, N, 8, 128), f32),
            pltpu.VMEM((8, 2, N, 8, 128), f32),
            pltpu.VMEM((2, TILE, B), f32),
            pltpu.VMEM((2, B, B), f32),
            pltpu.SemaphoreType.DMA((SEMS,)),
        ],
        compiler_params=pltpu.CompilerParams(
            collective_id=0, has_side_effects=True, vmem_limit_bytes=32 * 1024 * 1024
        ),
    )(*[pltpu.with_memory_space_constraint(value, pltpu.HBM) for value in (matrix, panels, factors)])


def solution(mesh):
    return jax.shard_map(
        per_device,
        mesh=mesh,
        in_specs=(P("row", "col"), P(None, ("col", "row"), None), P()),
        out_specs=P("row", "col"),
        check_vma=False,
    )
```

time: 122 us -> 103 us (0.84)
  Pallas kernels: 118 us -> 102 us
  local copies, waits for them, and re-layouts: 3.22 us -> 1.41 us
    pallas_call x1, Pallas kernels: 118 us -> 102 us  [per_device(): pl.pallas_call(kernel, out_shape=jax.ShapeDtypeStruct((TILE, TILE), f32),...]
    unnamed x1, local copies, waits for them, and re-layouts: 3.22 us -> 1.41 us
where the time goes in v2:
time: 103 us
  Pallas kernels  102 us (99%)
  local copies, waits for them, and re-layouts  1.41 us (1%)
    pallas_call x1, Pallas kernels, per_device(): pl.pallas_call(kernel, out_shape=jax.ShapeDtypeStruct((TILE, TILE), f32),...  102 us

profile of v2, /device:TPU:1, one launch (start us, length us, event | category | flops | bytes accessed | tf_op | source)
XLA Modules:
  0.0 103.3 jit_solution(17858402904864665707)
XLA Ops:
  0.0 101.9 %shard_map.37 = f32[768,768]{1,0:T(8,128)S(1)} custom-call(f32[768,768]{1,0:T(8,128)} %a_hbm.1, f32[2,48,256]{2,1,0:T(8,128)} %panels.1, f32[2,256,256]{2,1,0:T(8,128)} %f_hbm.1), custom_call_target="tpu_custom_call" | custom-call | tf_op jit(solution)/shard_map/pallas_call | solution.py:353
  101.9 1.4 %copy.5 = f32[768,768]{1,0:T(8,128)} copy(f32[768,768]{1,0:T(8,128)S(1)} %shard_map.37) | data formatting | bytes 4718592

commit v3 on v2

--- a/solution.py
+++ b/solution.py
@@ -314,13 +314,13 @@
     for state in rows_y:
         col_forward(state)
     ring_step(yc, ring, 3, unseen)
-    col_forward(rows_m)
-    ring_step(yc, ring, 4, unseen)
     for state in [rows_v] + rows_y:
         col_finish(state)
     for h in range(2):
         rows = slice(h * HALF, (h + 1) * HALF)
         a[rows, :] -= nt(row_panel(yr, 0, h), panel(0)) + nt(row_panel(yr, 1, h), panel(1))
+    col_forward(rows_m)
+    ring_step(yc, ring, 4, unseen)
     col_finish(rows_m)
 
     def block(i):

time: 103 us -> 103 us (level)
  no operation moved by 1% of the time
where the time goes in v3:
time: 103 us
  Pallas kernels  102 us (99%)
  local copies, waits for them, and re-layouts  1.41 us (1%)
    pallas_call x1, Pallas kernels, per_device(): pl.pallas_call(kernel, out_shape=jax.ShapeDtypeStruct((TILE, TILE), f32),...  102 us

profile of v3, /device:TPU:1, one launch (start us, length us, event | category | flops | bytes accessed | tf_op | source)
XLA Modules:
  0.0 103.0 jit_solution(16581771118795240757)
XLA Ops:
  0.0 101.6 %shard_map.37 = f32[768,768]{1,0:T(8,128)S(1)} custom-call(f32[768,768]{1,0:T(8,128)} %a_hbm.1, f32[2,48,256]{2,1,0:T(8,128)} %panels.1, f32[2,256,256]{2,1,0:T(8,128)} %f_hbm.1), custom_call_target="tpu_custom_call" | custom-call | tf_op jit(solution)/shard_map/pallas_call | solution.py:353
  101.6 1.4 %copy.5 = f32[768,768]{1,0:T(8,128)} copy(f32[768,768]{1,0:T(8,128)S(1)} %shard_map.37) | data formatting | bytes 4718592

commit v4 on v3

--- a/solution.py
+++ b/solution.py
@@ -252,13 +252,7 @@
     for copy in own_rows:
         copy.wait()
     rows_v = col_start(vr)
-    for copy in g_all:
-        copy.wait_recv()
-    for i in range(N):
-        bi, bj, s = i % 2, (i // 2) % 2, i // 4
-        gmat[128 * bi + 32 * s:128 * bi + 32 * s + 32, 128 * bj:128 * bj + 128] = gall[i]
     f1, f2 = f_ref[0], f_ref[1]
-    gf2 = nn(gmat[...], f2)
 
     def summed(p):
         for copy in parts[p * len(CHIPS):(p + 1) * len(CHIPS)]:
@@ -271,6 +265,12 @@
     first = nn(summed(0), f1)
     yr[chip, core, 0] = first
     turned_y = [Transpose(yr.at[chip, core, 0], yc.at[c, 0])]
+    for copy in g_all:
+        copy.wait_recv()
+    for i in range(N):
+        bi, bj, s = i % 2, (i // 2) % 2, i // 4
+        gmat[128 * bi + 32 * s:128 * bi + 32 * s + 32, 128 * bj:128 * bj + 128] = gall[i]
+    gf2 = nn(gmat[...], f2)
     second = nn(summed(1), f2) - nn(first, gf2)
     yr[chip, core, 1] = second
     turned_y.append(Transpose(yr.at[chip, core, 1], yc.at[c, 1]))

time: 103 us -> 102 us (level)
  no operation moved by 1% of the time
where the time goes in v4:
time: 102 us
  Pallas kernels  101 us (99%)
  local copies, waits for them, and re-layouts  1.41 us (1%)
    pallas_call x1, Pallas kernels, per_device(): pl.pallas_call(kernel, out_shape=jax.ShapeDtypeStruct((TILE, TILE), f32),...  101 us

profile of v4, /device:TPU:1, one launch (start us, length us, event | category | flops | bytes accessed | tf_op | source)
XLA Modules:
  0.0 102.2 jit_solution(1011226121437349051)
XLA Ops:
  0.0 100.8 %shard_map.37 = f32[768,768]{1,0:T(8,128)S(1)} custom-call(f32[768,768]{1,0:T(8,128)} %a_hbm.1, f32[2,48,256]{2,1,0:T(8,128)} %panels.1, f32[2,256,256]{2,1,0:T(8,128)} %f_hbm.1), custom_call_target="tpu_custom_call" | custom-call | tf_op jit(solution)/shard_map/pallas_call | solution.py:353
  100.8 1.4 %copy.5 = f32[768,768]{1,0:T(8,128)} copy(f32[768,768]{1,0:T(8,128)S(1)} %shard_map.37) | data formatting | bytes 4718592
